TPU v7x, 32 devices: a whole 2x2x4 slice. The times are simulated.
32 devices in a mesh: scan: 2 (over y), angle: 16 (over z, x, core).
Axes of the slice: x: 2, y: 2, z: 4, core: 2. Of those that a mesh axis runs over, the one named last changes fastest.
Arguments:
- object_init: float32 [32, 2, 128, 1024], P(('scan', 'angle')), parts along dimension 0, may hold values from -3.6 to 3.6
- measured: bfloat16 [32, 15, 128, 128], P(('scan', 'angle')), parts along dimension 0
- positions: int32 [32, 15, 2], P(('scan', 'angle')), parts along dimension 0, may hold values from 0 to 896, as said below
- angle_list: int32 [32], P('scan'), parts along dimension 0, may hold values from 0 to 15, each once
- probe: float32 [4, 128, 128], P('scan'), parts along dimension 0, may hold values from -3 to 3
- radial: float32 [16, 1024, 1024], P('angle'), may hold values from -0.1875 to 0.1875
Outputs:
- slices: float32 [32, 2, 128, 1024], P(('scan', 'angle')), parts along dimension 0
- probe_out: float32 [4, 128, 128], P('scan'), parts along dimension 0
There are 2 independent parts, one for each index of `scan`. A program takes and returns all parts, laid end to end along the dimension named above; an argument that names none is the same for every part. Nothing has to cross between parts.
Inputs may be any that keep to these rules, and one draw needn't show every extreme that they name: `positions`: for each angle, patch number n = r * 15 + c has offsets (r * 64, c * 64) moved by at most 8 cells in each dimension and clipped so that the patch lies inside the 128 x 1024 projection.
All inputs are finite; a program needn't handle non-finite values.
Results may differ from a plain program's by a relative error of at most 0.0014.
The roundings to bfloat16 on the way count: a program that leaves them out, or rounds other values in their place, can miss the bound.
Values sent between devices are 32-bit elements; how exact they have to be, the bound alone decides.
A program may use at most 64 MiB of HBM per device.

v0:
```python
import math
import jax
import jax.numpy as jnp
from jax import lax
from jax.sharding import PartitionSpec as P

ITERS = 2
object_rate = 0.5
probe_rate = 1.0


def tables_exact(count, index_list):
    index = jnp.arange(count, dtype=jnp.int32)
    phase = index[:, None] * index_list[None, :] % count
    angle = phase.astype(jnp.float32) * (2.0 * math.pi / count)
    scale = 1.0 / math.sqrt(count)
    return (jnp.cos(angle) * scale, jnp.sin(angle) * scale)


def tables(count, index_list):
    cosine_part, sine_part = tables_exact(count, index_list)
    return (cosine_part.astype(jnp.bfloat16), sine_part.astype(jnp.bfloat16))


def left(table, field):
    return jnp.einsum("jk,nkl->njl", table, field, preferred_element_type=jnp.float32)


def right(field, table):
    return jnp.einsum("njk,kl->njl", field, table, preferred_element_type=jnp.float32)


def gradient_list(
    object_field, measured_intensity, scan_positions, probe_field, cosine_theta, sine_theta
):
    size = probe_field.shape[1]
    zero_index = jnp.zeros((), jnp.int32)
    pieces = jax.vmap(
        lambda row, col: lax.dynamic_slice(object_field, (zero_index, row, col), (2, size, size))
    )(scan_positions[:, 0], scan_positions[:, 1])
    piece_re, piece_im = (pieces[:, 0], pieces[:, 1])
    probe_re, probe_im = (probe_field[0], probe_field[1])
    wave_re = (probe_re * piece_re - probe_im * piece_im).astype(jnp.bfloat16)
    wave_im = (probe_re * piece_im + probe_im * piece_re).astype(jnp.bfloat16)
    half_re = (left(cosine_theta, wave_re) + left(sine_theta, wave_im)).astype(jnp.bfloat16)
    half_im = (left(cosine_theta, wave_im) - left(sine_theta, wave_re)).astype(jnp.bfloat16)
    farfield_real = right(half_re, cosine_theta) + right(half_im, sine_theta)
    farfield_imaginary = right(half_im, cosine_theta) - right(half_re, sine_theta)
    residual_error = (
        farfield_real * farfield_real
        + farfield_imaginary * farfield_imaginary
        - measured_intensity.astype(jnp.float32)
    )
    push_re = (residual_error * farfield_real).astype(jnp.bfloat16)
    push_im = (residual_error * farfield_imaginary).astype(jnp.bfloat16)
    back_re = (left(cosine_theta, push_re) - left(sine_theta, push_im)).astype(jnp.bfloat16)
    back_im = (left(cosine_theta, push_im) + left(sine_theta, push_re)).astype(jnp.bfloat16)
    grad_re = right(back_re, cosine_theta) - right(back_im, sine_theta)
    grad_im = right(back_im, cosine_theta) + right(back_re, sine_theta)
    step_re = probe_re * grad_re + probe_im * grad_im
    step_im = probe_re * grad_im - probe_im * grad_re
    steps_all = jnp.stack([step_re, step_im], 1)

    def place(index, total):
        start = (zero_index, scan_positions[index, 0], scan_positions[index, 1])
        current = lax.dynamic_slice(total, start, (2, size, size))
        return lax.dynamic_update_slice(total, current + steps_all[index], start)

    obj_grad = lax.fori_loop(0, scan_positions.shape[0], place, jnp.zeros_like(object_field))
    pg_re = jnp.sum(piece_re * grad_re + piece_im * grad_im, 0)
    pg_im = jnp.sum(piece_re * grad_im - piece_im * grad_re, 0)
    energy = jnp.sum(piece_re * piece_re + piece_im * piece_im)
    return (obj_grad, jnp.stack([pg_re, pg_im], 0), energy)


def angular(block, wave_cos, wave_sin):
    count = block.shape[0]
    flat = block.reshape(count, -1)
    exact = lax.Precision.HIGHEST
    part_cos = jnp.dot(wave_cos, flat, precision=exact, preferred_element_type=jnp.float32).reshape(
        block.shape
    )
    part_sin = jnp.dot(wave_sin, flat, precision=exact, preferred_element_type=jnp.float32).reshape(
        block.shape
    )
    harm_re = part_cos[:, 0] + part_sin[:, 1]
    harm_im = part_cos[:, 1] - part_sin[:, 0]
    return jnp.stack([harm_re, harm_im], 1)


def on_device(object_init, measured, positions, angle_list, probe, radial):
    size = probe.shape[1]
    cosine_theta, sine_theta = tables(size, jnp.arange(size, dtype=jnp.int32))
    object_field = object_init
    probe_field = probe
    for step in range(ITERS):

        def one(items):
            return gradient_list(
                items[0], items[1], items[2], probe_field, cosine_theta, sine_theta
            )

        obj_grads, probe_grads, energies = lax.map(one, (object_field, measured, positions))
        probe_total, energy_total = lax.psum((jnp.sum(probe_grads, 0), jnp.sum(energies)), "angle")
        peak = jnp.max(probe_field[0] * probe_field[0] + probe_field[1] * probe_field[1])
        object_field = object_field - object_rate / peak * obj_grads
        probe_field = probe_field - probe_rate * probe_total / (energy_total / (size * size))
    wave_cos, wave_sin = tables_exact(angle_list.shape[0], angle_list)
    gathered = lax.all_to_all(object_field, "angle", split_axis=2, concat_axis=0, tiled=True)
    harm = lax.all_to_all(
        angular(gathered, wave_cos, wave_sin), "angle", split_axis=0, concat_axis=2, tiled=True
    )
    slices = jnp.einsum(
        "kcrn,knm->kcrm",
        harm,
        radial,
        precision=lax.Precision.HIGHEST,
        preferred_element_type=jnp.float32,
    )
    return (slices, probe_field)


def solution(mesh):
    in_specs = (
        P(("scan", "angle"), None, None, None),
        P(("scan", "angle"), None, None, None),
        P(("scan", "angle"), None, None),
        P("scan"),
        P("scan", None, None),
        P("angle", None, None),
    )
    out_specs = (P(("scan", "angle"), None, None, None), P("scan", None, None))
    return jax.shard_map(
        on_device, mesh=mesh, in_specs=in_specs, out_specs=out_specs, check_vma=False
    )
```

profile of v0, /device:TPU:8, one launch (start us, length us, event | category | flops | bytes accessed | tf_op | source)
XLA Modules:
  0.0 385.9 jit_solution(10983038799125892460)
XLA Ops:
  7.2 0.8 fusion.125
  8.0 1.5 copy.167
  9.5 2.7 gather_fusion
  12.3 3.3 fusion.297
  15.6 2.3 copy.237
  17.9 2.7 copy.238
  24.7 0.7 multiply_convert_fusion.2
  29.2 3.0 fusion.42
  32.9 0.7 add_reduce_fusion.1
  33.6 3.0 pad_maximum_fusion
  36.9 67.4 %while.44 = (s32[]{:T(128)}, f32[2,128,1024]{1,0,2:T(2,128)S(1)}, s32[15,2]{0,1:T(2,128)S(1)}, f32[15,2,128,128]{3,2,0,1:T(8,128)}, s32[]{:T(128)}, /*index=5*/s32[]{:T(128)}, s32[]{:T(128)}) while((s32[]{:T(128)}, f32[2,128,1024]{1,0,2:T(2,128)S(1)}, s32[15,2]{0,1:T(2,128)S(1)}, f32[15,2,128,128]{3,2,0,1:T(8,128)}, s32[]{:T(128)}, ...), condition=%wide.region_2.3_spmd, body=%wide.region_1.2_spmd.sunk | while | flops 32773 | bytes 1441927 | solution.py:69
  39.6 0.9 bitcast_add_fusion.4
  43.3 0.9 bitcast_add_fusion.4
  47.1 0.9 bitcast_add_fusion.4
  50.8 0.9 bitcast_add_fusion.4
  54.6 0.9 bitcast_add_fusion.4
  58.3 0.9 bitcast_add_fusion.4
  62.1 0.9 bitcast_add_fusion.4
  65.8 0.9 bitcast_add_fusion.4
  69.6 0.9 bitcast_add_fusion.4
  73.3 0.9 bitcast_add_fusion.4
  77.1 0.9 bitcast_add_fusion.4
  80.8 0.9 bitcast_add_fusion.4
  84.6 0.9 bitcast_add_fusion.4
  88.3 0.9 bitcast_add_fusion.4
  92.1 0.9 bitcast_add_fusion.4
  105.5 3.9 %gather_fusion.1 = f32[15,2,128,128]{2,1,3,0:T(2,128)} fusion(f32[2,128,1024]{1,0,2:T(2,128)S(1)} %fusion.103, s32[15]{0:T(128)S(1)} %fusion.125), kind=kCustom, calls=%fused_computation.1 | custom fusion | bytes 3932340 | tf_op jit(solution)/shard_map/while/body/eval_jaxpr/vmap()/gather | solution.py:39
  109.5 5.4 %fusion.296 = (f32[15,1,128,128]{2,1,3,0:T(1,128)}, f32[15,1,128,128]{2,1,3,0:T(1,128)}) fusion(f32[15,2,128,128]{2,1,3,0:T(2,128)} %gather_fusion.1), kind=kLoop, calls=%fused_computation.344 | loop fusion | bytes 3932160 | tf_op jit(solution)/shard_map/while/body/eval_jaxpr/slice | solution.py:41
  114.9 26.1 %psum.29 = f32[]{:T(128)} all-reduce(f32[]{:T(128)} %get-tuple-element.271), channel_id=1, replica_groups=mesh['scan'=2,'angle'=16] {'angle'}, use_global_device_ids=true, to_apply=%region_7.8 | all-reduce | flops 1 | bytes 8 | tf_op jit(solution)/shard_map/psum | solution.py:104
  141.1 2.3 copy.239
  143.3 3.2 copy.240
  147.3 0.9 divide_subtract_fusion.1
  148.8 1.5 fusion.30
  154.1 0.7 multiply_convert_fusion
  158.7 1.8 fusion.32
  160.5 1.5 pad_maximum_fusion.1
  162.3 56.3 %while.45 = (s32[]{:T(128)}, f32[2,128,1024]{1,0,2:T(2,128)S(1)}, s32[15,2]{0,1:T(2,128)S(1)}, f32[15,2,128,128]{3,2,0,1:T(8,128)}, s32[]{:T(128)}, /*index=5*/s32[]{:T(128)}, s32[]{:T(128)}) while((s32[]{:T(128)}, f32[2,128,1024]{1,0,2:T(2,128)S(1)}, s32[15,2]{0,1:T(2,128)S(1)}, f32[15,2,128,128]{3,2,0,1:T(8,128)}, s32[]{:T(128)}, ...), condition=%wide.region_10.11_spmd, body=%wide.region_9.10_spmd.sunk | while | flops 32773 | bytes 1441927 | solution.py:69
  164.9 0.9 bitcast_add_fusion.5
  168.7 0.9 bitcast_add_fusion.5
  172.5 0.9 bitcast_add_fusion.5
  176.2 0.9 bitcast_add_fusion.5
  180.0 0.9 bitcast_add_fusion.5
  183.7 0.9 bitcast_add_fusion.5
  187.5 0.9 bitcast_add_fusion.5
  191.2 0.9 bitcast_add_fusion.5
  195.0 0.9 bitcast_add_fusion.5
  198.7 0.9 bitcast_add_fusion.5
  202.5 0.9 bitcast_add_fusion.5
  206.2 0.9 bitcast_add_fusion.5
  210.0 0.9 bitcast_add_fusion.5
  213.7 0.9 bitcast_add_fusion.5
  217.5 0.9 bitcast_add_fusion.5
  219.1 1.7 bitcast_subtract_fusion
  220.8 2.4 copy.188
  223.3 35.7 %all_to_all.30 = f32[1,2,128,1024]{3,1,0,2:T(2,128)S(1)} all-to-all(f32[1,2,128,1024]{3,1,0,2:T(2,128)S(1)} %copy.188), channel_id=1, replica_groups=mesh['scan'=2,'angle'=16] {'angle'}, dimensions={2} | all-to-all | bytes 2097152 | tf_op jit(solution)/shard_map/all_to_all | solution.py:109
  260.2 1.5 fusion.23
  261.8 1.5 fusion.25
  263.6 1.6 copy.193
  265.2 4.9 %all-to-all-start.1 = ((f32[16,2,8,1024]{3,2,1,0:T(8,128)}), f32[16,2,8,1024]{3,2,1,0:T(8,128)S(1)}, u32[]{:S(2)}, u32[]{:S(2)}) async-start(f32[16,2,8,1024]{3,2,1,0:T(8,128)} %copy.193), calls=%async_computation.1 | async-start | bytes 2097152 | tf_op jit(solution)/shard_map/all_to_all | solution.py:110
  270.1 0.7 pad_maximum_fusion.4
  270.8 40.6 %psum.31 = f32[]{:T(128)} all-reduce(f32[]{:T(128)} %get-tuple-element.270), channel_id=1, replica_groups=mesh['scan'=2,'angle'=16] {'angle'}, use_global_device_ids=true, to_apply=%region_15.16 | all-reduce | flops 1 | bytes 8 | tf_op jit(solution)/shard_map/psum | solution.py:104
  312.0 58.5 %all-reduce.5.cloned.1.call-done = f32[2,128,128]{2,1,0:T(8,128)} async-done(((f32[2,128,128]{2,1,0:T(8,128)}), f32[2,128,128]{2,1,0:T(8,128)}) %all-reduce.5.cloned.1.call-update) | async-done | bytes 131088 | tf_op jit(solution)/shard_map/psum | solution.py:104
  370.5 1.6 divide_subtract_fusion
  372.1 6.8 %fusion.2 = f32[1,2,128,1024]{3,2,1,0:T(8,128)} fusion(f32[1,1024,1024]{2,1,0:T(8,128)} %param.15, f32[16,2,8,1024]{3,2,1,0:T(8,128)S(1)} %all-to-all-done.1), kind=kOutput, calls=%fused_computation.14 | convolution fusion | flops 3221225472 | bytes 6291456 | tf_op jit(solution)/shard_map/kcrn,knm->kcrm/dot_general | solution.py:113
  (214 shorter events, 44.2 us)
Async XLA Ops:
  7.2 140.1 %all-reduce.3.cloned.1.call-start = ((), (), s32[]{:S(2)}) async-start(), calls=%async_computation.2 | async-start | bytes 262144 | tf_op jit(solution)/shard_map/psum | solution.py:104
  15.6 5.0 %copy-start.3 = (f32[2,128,128]{2,1,0:T(8,128)S(1)}, f32[2,128,128]{2,1,0:T(8,128)}, u32[]{:S(2)}) copy-start(f32[2,128,128]{2,1,0:T(8,128)} %param.14) | copy-start | bytes 393220
  23.6 1.1 copy-start.1
  33.6 3.3 copy-start.7
  153.0 1.1 copy-start.2
  157.5 1.2 copy-start
  259.4 0.8 copy-start.6
  263.6 6.5 %copy-start.4 = (f32[128,128]{1,0:T(8,128)S(1)}, f32[128,128]{1,0:T(8,128)}, u32[]{:S(2)}) copy-start(f32[128,128]{1,0:T(8,128)} %get-tuple-element.266) | copy-start | bytes 196612
  263.6 6.5 %copy-start.5 = (f32[128,128]{1,0:T(8,128)S(1)}, f32[128,128]{1,0:T(8,128)}, u32[]{:S(2)}) copy-start(f32[128,128]{1,0:T(8,128)} %get-tuple-element.267) | copy-start | bytes 196612
  265.2 106.9 %all-to-all-start.1 = ((f32[16,2,8,1024]{3,2,1,0:T(8,128)}), f32[16,2,8,1024]{3,2,1,0:T(8,128)S(1)}, u32[]{:S(2)}, u32[]{:S(2)}) async-start(f32[16,2,8,1024]{3,2,1,0:T(8,128)} %copy.193), calls=%async_computation.1 | async-start | bytes 2097152 | tf_op jit(solution)/shard_map/all_to_all | solution.py:110
  270.0 100.4 %all-reduce.5.cloned.1.call-start = ((), (), s32[]{:S(2)}) async-start(), calls=%async_computation.3 | async-start | bytes 262144 | tf_op jit(solution)/shard_map/psum | solution.py:104
Sparse Core Ops, SparseCore 0:
  33.0 92.0 all-reduce.2
  274.9 95.5 all-reduce.4
where the time goes:
time: 393 us; the launch traced here: 386 us
  blocking collectives  102 us (26%)
  loops' own time  70.8 us (18%)
  waiting for transfers between devices  58.6 us (15%)
  local copies, waits for them, and re-layouts  58.4 us (15%)
  other arithmetic  42.5 us (11%)
  matrix products  31.1 us (8%)
  between operations  17.3 us (4%)
  starting transfers between devices  4.94 us (1%)
    another operation x2, loops' own time, gradient_list(): lax.fori_loop(0, scan_positions.shape[0], place, jnp.zeros_like(object_fi...  70.8 us
    psum x2, blocking collectives, on_device(): lax.psum((jnp.sum(probe_grads, 0), jnp.sum(energies)), 'angle')  66.7 us
    psum x2, waiting for transfers between devices, on_device(): lax.psum((jnp.sum(probe_grads, 0), jnp.sum(energies)), 'angle')  58.5 us
    all_to_all x1, blocking collectives, on_device(): lax.all_to_all(object_field, 'angle', split_axis=2, concat_axis=0, tiled=...  35.7 us
    add x30, other arithmetic, place(): return lax.dynamic_update_slice(total, current + steps_all[index], start)  27.9 us
    dynamic_slice x30, local copies, waits for them, and re-layouts, place(): start = (zero_index, scan_positions[index, 0], scan_positions[index, 1])  17.5 us
    unnamed x22, local copies, waits for them, and re-layouts  12.8 us
    dot_general x16, matrix products, right(): jnp.einsum('njk,kl->njl', field, table, preferred_element_type=jnp.float32)  12.7 us
  transfers between devices with their start and end apart: 3, of which 1 were waited for; matrix products, arithmetic and copies ran while one was open for 12% of the time, Pallas kernels for 0%

commit v1 on v0

--- a/solution.py
+++ b/solution.py
@@ -106,7 +106,12 @@
         object_field = object_field - object_rate / peak * obj_grads
         probe_field = probe_field - probe_rate * probe_total / (energy_total / (size * size))
     wave_cos, wave_sin = tables_exact(angle_list.shape[0], angle_list)
-    gathered = lax.all_to_all(object_field, "angle", split_axis=2, concat_axis=0, tiled=True)
+    gathered = jnp.concatenate(
+        lax.all_to_all(
+            jnp.stack(jnp.split(object_field, lax.axis_size("angle"), axis=2)), "angle", 0, 0
+        ),
+        axis=0,
+    )
     harm = lax.all_to_all(
         angular(gathered, wave_cos, wave_sin), "angle", split_axis=0, concat_axis=2, tiled=True
     )

time: 393 us -> 423 us (1.076)
  local copies, waits for them, and re-layouts: 58.4 us -> 100 us
  loops' own time: 70.8 us -> 59.9 us
    another operation x2 -> x20, local copies, waits for them, and re-layouts: 0.54 us -> 44.8 us  [the longest x18 44.3 us: on_device(): jnp.stack(jnp.split(object_field, lax.axis_size('angle'), axis=2))]
    another operation x2, loops' own time: 70.8 us -> 59.9 us  [gradient_list(): lax.fori_loop(0, scan_positions.shape[0], place, jnp.zeros_like(object_fi...]
    unnamed x22 -> x56, local copies, waits for them, and re-layouts: 12.8 us -> 12.4 us
where the time goes in v1:
time: 423 us; the launch traced here: 416 us
  blocking collectives  102 us (24%)
  local copies, waits for them, and re-layouts  100 us (24%)
  loops' own time  59.9 us (14%)
  waiting for transfers between devices  58.6 us (14%)
  other arithmetic  41.6 us (10%)
  matrix products  31.1 us (7%)
  between operations  17.7 us (4%)
  starting transfers between devices  4.98 us (1%)
    psum x2, blocking collectives, on_device(): lax.psum((jnp.sum(probe_grads, 0), jnp.sum(energies)), 'angle')  66.6 us
    another operation x2, loops' own time, gradient_list(): lax.fori_loop(0, scan_positions.shape[0], place, jnp.zeros_like(object_fi...  59.9 us
    psum x2, waiting for transfers between devices, on_device(): lax.psum((jnp.sum(probe_grads, 0), jnp.sum(energies)), 'angle')  58.5 us
    another operation x18, local copies, waits for them, and re-layouts, on_device(): jnp.stack(jnp.split(object_field, lax.axis_size('angle'), axis=2))  44.3 us
    all_to_all x1, blocking collectives, on_device(): lax.all_to_all(jnp.stack(jnp.split(object_field, lax.axis_size('angle'),...  35.7 us
    add x30, other arithmetic, place(): return lax.dynamic_update_slice(total, current + steps_all[index], start)  27.9 us
    dynamic_slice x30, local copies, waits for them, and re-layouts, place(): start = (zero_index, scan_positions[index, 0], scan_positions[index, 1])  17.5 us
    dot_general x16, matrix products, right(): jnp.einsum('njk,kl->njl', field, table, preferred_element_type=jnp.float32)  12.7 us
  transfers between devices with their start and end apart: 3, of which 1 were waited for; matrix products, arithmetic and copies ran while one was open for 12% of the time, Pallas kernels for 0%

profile of v1, /device:TPU:8, one launch (start us, length us, event | category | flops | bytes accessed | tf_op | source)
XLA Modules:
  0.0 416.2 jit_solution(13064165628303111224)
XLA Ops:
  8.9 1.5 copy.117
  10.4 2.7 gather_fusion
  13.2 3.3 fusion.297
  16.5 2.3 copy.200
  18.8 2.8 copy.201
  30.2 3.1 fusion.42
  34.6 3.0 pad_maximum_fusion
  37.9 56.5 %while.44 = (s32[]{:T(128)}, f32[2,128,1024]{1,0,2:T(2,128)S(1)}, s32[15,2]{0,1:T(2,128)S(1)}, f32[15,2,128,128]{3,2,0,1:T(8,128)}, s32[]{:T(128)}, /*index=5*/s32[]{:T(128)}, s32[]{:T(128)}) while((s32[]{:T(128)}, f32[2,128,1024]{1,0,2:T(2,128)S(1)}, s32[15,2]{0,1:T(2,128)S(1)}, f32[15,2,128,128]{3,2,0,1:T(8,128)}, s32[]{:T(128)}, ...), condition=%wide.region_2.3_spmd, body=%wide.region_1.2_spmd.sunk | while | flops 32773 | bytes 1441935 | solution.py:69
  40.6 0.9 bitcast_add_fusion.4
  44.3 0.9 bitcast_add_fusion.4
  48.1 0.9 bitcast_add_fusion.4
  51.9 0.9 bitcast_add_fusion.4
  55.6 0.9 bitcast_add_fusion.4
  59.4 0.9 bitcast_add_fusion.4
  63.1 0.9 bitcast_add_fusion.4
  66.9 0.9 bitcast_add_fusion.4
  70.6 0.9 bitcast_add_fusion.4
  74.4 0.9 bitcast_add_fusion.4
  78.1 0.9 bitcast_add_fusion.4
  81.9 0.9 bitcast_add_fusion.4
  85.6 0.9 bitcast_add_fusion.4
  89.4 0.9 bitcast_add_fusion.4
  93.1 0.9 bitcast_add_fusion.4
  95.7 4.0 gather_fusion.1
  99.6 5.4 %fusion.296 = (f32[15,1,128,128]{2,1,3,0:T(1,128)}, f32[15,1,128,128]{2,1,3,0:T(1,128)}) fusion(f32[15,2,128,128]{2,1,3,0:T(2,128)} %gather_fusion.1), kind=kLoop, calls=%fused_computation.375 | loop fusion | bytes 3932160 | tf_op jit(solution)/shard_map/while/body/eval_jaxpr/slice | solution.py:41
  105.0 26.1 %psum.29 = f32[]{:T(128)} all-reduce(f32[]{:T(128)} %get-tuple-element.263), channel_id=1, replica_groups=mesh['scan'=2,'angle'=16] {'angle'}, use_global_device_ids=true, to_apply=%region_7.8 | all-reduce | flops 1 | bytes 8 | tf_op jit(solution)/shard_map/psum | solution.py:104
  131.2 2.3 copy.202
  133.5 3.2 copy.203
  139.6 1.5 fusion.30
  149.5 1.8 fusion.32
  151.3 1.5 pad_maximum_fusion.1
  153.1 56.3 %while.45 = (s32[]{:T(128)}, f32[2,128,1024]{1,0,2:T(2,128)S(1)}, s32[15,2]{0,1:T(2,128)S(1)}, f32[15,2,128,128]{3,2,0,1:T(8,128)}, s32[]{:T(128)}, /*index=5*/s32[]{:T(128)}, s32[]{:T(128)}) while((s32[]{:T(128)}, f32[2,128,1024]{1,0,2:T(2,128)S(1)}, s32[15,2]{0,1:T(2,128)S(1)}, f32[15,2,128,128]{3,2,0,1:T(8,128)}, s32[]{:T(128)}, ...), condition=%wide.region_10.11_spmd, body=%wide.region_9.10_spmd.sunk | while | flops 32773 | bytes 1441935 | solution.py:69
  155.7 0.9 bitcast_add_fusion.5
  159.5 0.9 bitcast_add_fusion.5
  163.2 0.9 bitcast_add_fusion.5
  167.0 0.9 bitcast_add_fusion.5
  170.7 0.9 bitcast_add_fusion.5
  174.5 0.9 bitcast_add_fusion.5
  178.2 0.9 bitcast_add_fusion.5
  182.0 0.9 bitcast_add_fusion.5
  210.1 18.9 %slice_bitcast_fusion = (f32[1,1,2,8,1024]{3,2,4,1,0:T(2,128)}, f32[1,1,2,8,1024]{3,2,4,1,0:T(2,128)}, f32[1,1,2,8,1024]{3,2,4,1,0:T(2,128)}, f32[1,1,2,8,1024]{...) fusion(f32[1,2,128,1024]{2,1,3,0:T(2,128)S(1)} %bitcast_subtrac, ...), kind=kLoop, calls=%fused_computation.49 | loop fusion | bytes 2097152 | tf_op jit(solution)/shard_map/stack | solution.py:111
  229.0 1.4 copy.153
  230.4 1.4 copy.152
  231.8 1.4 copy.151
  233.1 1.4 copy.150
  234.5 2.0 copy.149
  236.5 2.0 copy.148
  238.5 2.0 copy.147
  240.5 2.0 copy.146
  242.5 2.0 copy.145
  244.5 2.0 copy.144
  246.5 2.0 copy.143
  248.5 2.0 copy.142
  250.5 2.0 copy.141
  252.5 1.0 copy.140
  254.8 35.7 %all_to_all.20 = f32[16,1,2,8,1024]{4,3,2,1,0:T(8,128)S(1)} all-to-all(f32[16,1,2,8,1024]{4,3,2,1,0:T(8,128)S(1)} %constant_dynamic-update-slice_fusion.2), channel_id=1, replica_groups=mesh['scan'=2,'angle'=16] {'angle'}, dimensions={0} | all-to-all | bytes 2097152 | tf_op jit(solution)/shard_map/all_to_all | solution.py:110
  290.5 1.5 fusion.23
  292.0 1.5 fusion.25
  293.8 1.6 copy.156
  295.4 4.9 %all-to-all-start.1 = ((f32[16,2,8,1024]{3,2,1,0:T(8,128)}), f32[16,2,8,1024]{3,2,1,0:T(8,128)S(1)}, u32[]{:S(2)}, u32[]{:S(2)}) async-start(f32[16,2,8,1024]{3,2,1,0:T(8,128)} %copy.156), calls=%async_computation.1 | async-start | bytes 2097152 | tf_op jit(solution)/shard_map/all_to_all | solution.py:115
  301.1 40.4 %psum.31 = f32[]{:T(128)} all-reduce(f32[]{:T(128)} %get-tuple-element.262), channel_id=1, replica_groups=mesh['scan'=2,'angle'=16] {'angle'}, use_global_device_ids=true, to_apply=%region_15.16 | all-reduce | flops 1 | bytes 8 | tf_op jit(solution)/shard_map/psum | solution.py:104
  342.2 58.5 %all-reduce.5.cloned.1.call-done = f32[2,128,128]{2,1,0:T(8,128)} async-done(((f32[2,128,128]{2,1,0:T(8,128)}), f32[2,128,128]{2,1,0:T(8,128)}) %all-reduce.5.cloned.1.call-update) | async-done | bytes 131088 | tf_op jit(solution)/shard_map/psum | solution.py:104
  400.7 1.6 divide_subtract_fusion
  402.2 6.8 %fusion.2 = f32[1,2,128,1024]{3,2,1,0:T(8,128)} fusion(f32[1,1024,1024]{2,1,0:T(8,128)} %param.15, f32[16,2,8,1024]{3,2,1,0:T(8,128)S(1)} %all-to-all-done.1), kind=kOutput, calls=%fused_computation.14 | convolution fusion | flops 3221225472 | bytes 6291456 | tf_op jit(solution)/shard_map/kcrn,knm->kcrm/dot_general | solution.py:118
  (262 shorter events, 56.6 us)
Async XLA Ops:
  7.2 130.2 %all-reduce.3.cloned.1.call-start = ((), (), s32[]{:S(2)}) async-start(), calls=%async_computation.2 | async-start | bytes 262144 | tf_op jit(solution)/shard_map/psum | solution.py:104
  24.6 1.1 copy-start.1
  30.2 3.8 copy-start.3
  34.6 3.3 copy-start.17
  143.7 1.1 copy-start.2
  148.3 1.2 copy-start
  253.5 0.9 copy-start.15
  253.6 1.0 copy-start.14
  253.6 1.0 copy-start.13
  253.6 1.0 copy-start.12
  253.6 1.0 copy-start.11
  253.6 1.1 copy-start.10
  253.6 1.1 copy-start.9
  253.6 1.1 copy-start.8
  253.6 1.1 copy-start.7
  253.6 1.1 copy-start.6
  254.5 36.0 %copy-start.16 = (s32[16]{0:T(128)S(1)}, s32[16]{0:T(128)}, u32[]{:S(2)}) copy-start(s32[16]{0:T(128)} %param.13) | copy-start | bytes 196
  293.8 6.6 %copy-start.4 = (f32[128,128]{1,0:T(8,128)S(1)}, f32[128,128]{1,0:T(8,128)}, u32[]{:S(2)}) copy-start(f32[128,128]{1,0:T(8,128)} %get-tuple-element.258) | copy-start | bytes 196612
  293.8 6.6 %copy-start.5 = (f32[128,128]{1,0:T(8,128)S(1)}, f32[128,128]{1,0:T(8,128)}, u32[]{:S(2)}) copy-start(f32[128,128]{1,0:T(8,128)} %get-tuple-element.259) | copy-start | bytes 196612
  295.4 106.8 %all-to-all-start.1 = ((f32[16,2,8,1024]{3,2,1,0:T(8,128)}), f32[16,2,8,1024]{3,2,1,0:T(8,128)S(1)}, u32[]{:S(2)}, u32[]{:S(2)}) async-start(f32[16,2,8,1024]{3,2,1,0:T(8,128)} %copy.156), calls=%async_computation.1 | async-start | bytes 2097152 | tf_op jit(solution)/shard_map/all_to_all | solution.py:115
  300.3 100.3 %all-reduce.5.cloned.1.call-start = ((), (), s32[]{:S(2)}) async-start(), calls=%async_computation.3 | async-start | bytes 262144 | tf_op jit(solution)/shard_map/psum | solution.py:104
Sparse Core Ops, SparseCore 0:
  34.0 92.0 all-reduce.2
  305.2 95.4 all-reduce.4
